TPU v7x, 32 devices: a whole 2x2x4 slice. The times are simulated.
32 devices in a mesh: dp: 8 (over y, x, core), tensor: 4 (over z).
Axes of the slice: x: 2, y: 2, z: 4, core: 2. Of those that a mesh axis runs over, the one named last changes fastest.
Arguments:
- block_input: bfloat16 [8192, 2048], P('dp'), may hold values from -24 to 24
- segments: int32 [8192], P('dp'), may hold values from 0 to 15, never falling along the last dimension, each value on 1 to 2048 neighbouring positions
- norm_gain: bfloat16 [2048], P('dp'), may hold values from 0.5 to 1.5
- norm_bias: bfloat16 [2048], P('dp'), may hold values from -1.75 to 1.75
- qkv_weight: bfloat16 [2048, 3, 2048], P('dp', None, 'tensor'), may hold values from -1 to 1
- query_value_bias: bfloat16 [2, 32, 64], P(None, 'tensor', 'dp'), may hold values from -1.75 to 1.75
- key_bias: bfloat16 [32, 32], P('tensor', 'dp'), may hold values from -3 to 3
- dense_weight: bfloat16 [2048, 2048], P('tensor', 'dp'), may hold values from -1.5 to 1.5
- dense_bias: bfloat16 [2048], P('dp'), may hold values from -1.75 to 1.75
- up_weight: bfloat16 [2048, 8192], P('dp', 'tensor'), may hold values from -0.125 to 0.125
- up_bias: bfloat16 [128, 64], P('tensor', 'dp'), may hold values from -1.75 to 1.75
- down_weight: bfloat16 [8192, 2048], P('tensor', 'dp'), may hold values from -0.0625 to 0.0625
- down_bias: bfloat16 [2048], P('dp'), may hold values from -1.75 to 1.75
- cotangent: bfloat16 [8192, 2048], P('dp'), may hold values from -8 to 8
Outputs:
- block_output: bfloat16 [8192, 2048], P('dp')
- input_grad: float32 [8192, 2048], P('dp')
- norm_gain_grad: float32 [2048], P('dp')
- norm_bias_grad: float32 [2048], P('dp')
- qkv_weight_grad: float32 [2048, 3, 2048], P('dp', None, 'tensor')
- query_value_bias_grad: float32 [2, 32, 64], P(None, 'tensor', 'dp')
- key_bias_grad: float32 [32, 32], P('tensor', 'dp')
- dense_weight_grad: float32 [2048, 2048], P('tensor', 'dp')
- dense_bias_grad: float32 [2048], P('dp')
- up_weight_grad: float32 [2048, 8192], P('dp', 'tensor')
- up_bias_grad: float32 [128, 64], P('tensor', 'dp')
- down_weight_grad: float32 [8192, 2048], P('tensor', 'dp')
- down_bias_grad: float32 [2048], P('dp')
Inputs may be any that keep to these rules, and one draw needn't show every extreme that they name: `segments`: segment numbers never fall along the tokens; each segment has 1 to 2048 tokens, one exactly 2048.
All inputs are finite; a program needn't handle non-finite values.
Results may differ from a plain program's by a relative error of at most 0.015.
The roundings to bfloat16 on the way count: a program that leaves them out, or rounds other values in their place, can miss the bound.
Values may be sent and summed in bfloat16 or wider, within the bound.
A program may use at most 256 MiB of HBM per device.

v0:
```python
import math
import jax
import jax.numpy as jnp
from jax import lax
from jax.sharding import PartitionSpec as P

HEAD = 64
ROT = 32
SEQ = 512
EPSILON = 1e-05
SCALE = 0.125
NEGATIVE = -1e30


def rotary_tables(seg_rows):
    seq_len = seg_rows.shape[1]
    position = jnp.arange(seq_len, dtype=jnp.int32)
    starting = jnp.concatenate(
        [jnp.ones((seg_rows.shape[0], 1), dtype=jnp.bool_), seg_rows[:, 1:] != seg_rows[:, :-1]],
        axis=1,
    )
    starts = lax.cummax(jnp.where(starting, position[None, :], jnp.int32(0)), axis=1)
    offset = (position[None, :] - starts).astype(jnp.float32)
    halfway = ROT // 2
    inverse = 10000.0 ** (-(jnp.arange(halfway, dtype=jnp.float32) * (2.0 / ROT)))
    angles = offset[:, :, None] * inverse
    return (jnp.cos(angles), jnp.sin(angles))


def rotate(tensor, cosine_table, sine_table, direction):
    halfway = ROT // 2
    leading = tensor[..., :halfway]
    trailing = tensor[..., halfway:ROT]
    others = tensor[..., ROT:]
    cosine_part = cosine_table[:, :, None, :]
    sine_part = sine_table[:, :, None, :] * direction
    return jnp.concatenate(
        [
            leading * cosine_part - trailing * sine_part,
            trailing * cosine_part + leading * sine_part,
            others,
        ],
        axis=-1,
    )


def allowed_pairs(seg_rows):
    seq_len = seg_rows.shape[1]
    position = jnp.arange(seq_len, dtype=jnp.int32)
    causal = position[:, None] >= position[None, :]
    same_doc = seg_rows[:, :, None] == seg_rows[:, None, :]
    return (same_doc & causal[None])[:, None]


def gelu_tanh(inputs):
    return jax.nn.gelu(inputs, approximate=True)


def masked_scores(queries, key_rows, allowed):
    scores = (
        jnp.einsum("nqhd,nkhd->nhqk", queries, key_rows, preferred_element_type=jnp.float32) * SCALE
    )
    return jnp.where(allowed, scores, NEGATIVE)


def attend_group(placeholder, inputs):
    queries, key_rows, values, allowed = inputs
    scores = masked_scores(queries, key_rows, allowed)
    row_max = jnp.max(scores, axis=-1, keepdims=True)
    row_total = jnp.sum(jnp.exp(scores - row_max), axis=-1, keepdims=True)
    log_total = row_max + jnp.log(row_total)
    prob_low = jnp.exp(scores - log_total).astype(jnp.bfloat16)
    mixed_part = jnp.einsum(
        "nhqk,nkhd->nqhd", prob_low, values, preferred_element_type=jnp.float32
    ).astype(jnp.bfloat16)
    return (placeholder, (mixed_part, log_total))


def attend_back_group(placeholder, inputs):
    queries, key_rows, values, allowed, log_total, grad_mixed = inputs
    scores = masked_scores(queries, key_rows, allowed)
    probabilities = jnp.exp(scores - log_total)
    prob_low = probabilities.astype(jnp.bfloat16)
    grad_values = jnp.einsum(
        "nhqk,nqhd->nkhd", prob_low, grad_mixed, preferred_element_type=jnp.float32
    )
    grad_probs = jnp.einsum(
        "nqhd,nkhd->nhqk", grad_mixed, values, preferred_element_type=jnp.float32
    )
    row_delta = jnp.sum(probabilities * grad_probs, axis=-1, keepdims=True)
    grad_scores = (probabilities * (grad_probs - row_delta) * SCALE).astype(jnp.bfloat16)
    grad_queries = jnp.einsum(
        "nhqk,nkhd->nqhd", grad_scores, key_rows, preferred_element_type=jnp.float32
    )
    grad_keys = jnp.einsum(
        "nhqk,nqhd->nkhd", grad_scores, queries, preferred_element_type=jnp.float32
    )
    return (placeholder, (grad_queries, grad_keys, grad_values))


def local(
    block_input,
    segments,
    norm_gain,
    norm_bias,
    qkv_weight,
    query_value_bias,
    key_bias,
    dense_weight,
    dense_bias,
    up_weight,
    up_bias,
    down_weight,
    down_bias,
    cotangent,
):
    gathered = (
        lax.all_gather(norm_gain, "dp", axis=0, tiled=True),
        lax.all_gather(norm_bias, "dp", axis=0, tiled=True),
        lax.all_gather(qkv_weight, "dp", axis=0, tiled=True),
        lax.all_gather(query_value_bias, "dp", axis=2, tiled=True),
        lax.all_gather(key_bias, "dp", axis=1, tiled=True),
        lax.all_gather(dense_weight, "dp", axis=1, tiled=True),
        lax.all_gather(dense_bias, "dp", axis=0, tiled=True),
        lax.all_gather(up_weight, "dp", axis=0, tiled=True),
        lax.all_gather(up_bias, "dp", axis=1, tiled=True),
        lax.all_gather(down_weight, "dp", axis=1, tiled=True),
        lax.all_gather(down_bias, "dp", axis=0, tiled=True),
    )
    (
        gain_all,
        shift_all,
        qkv_all,
        qv_all,
        key_all,
        dense_all,
        dense_shift_all,
        up_all,
        up_shift_all,
        down_all,
        down_shift_all,
    ) = gathered
    row_count, model_width = block_input.shape
    local_width = qkv_all.shape[2]
    heads_here = local_width // HEAD
    seqs_here = row_count // SEQ
    per_step = math.gcd(seqs_here, max(1, 512 // SEQ))
    groups = seqs_here // per_step

    def to_groups(tensor):
        return tensor.reshape((groups, per_step) + tensor.shape[1:])

    def from_groups(tensor):
        return tensor.reshape((seqs_here,) + tensor.shape[2:])

    widened = block_input.astype(jnp.float32)
    row_mean = jnp.mean(widened, axis=1, keepdims=True)
    centred = widened - row_mean
    row_var = jnp.mean(centred * centred, axis=1, keepdims=True)
    inv_std = lax.rsqrt(row_var + EPSILON)
    normed = centred * inv_std
    normed_low = (normed * gain_all.astype(jnp.float32) + shift_all.astype(jnp.float32)).astype(
        jnp.bfloat16
    )
    qkv_flat = qkv_all.reshape(model_width, 3 * local_width)
    projected = jnp.dot(normed_low, qkv_flat, preferred_element_type=jnp.float32).reshape(
        seqs_here, SEQ, 3, heads_here, HEAD
    )
    seq_segs = segments.reshape(seqs_here, SEQ)
    cosine_table, sine_table = rotary_tables(seq_segs)
    allowed = allowed_pairs(seq_segs)
    qv_wide = qv_all.astype(jnp.float32)
    key_full = jnp.concatenate(
        [key_all.astype(jnp.float32), jnp.zeros((heads_here, HEAD - ROT), jnp.float32)], axis=1
    )
    queries = rotate(projected[:, :, 0] + qv_wide[0], cosine_table, sine_table, 1.0).astype(
        jnp.bfloat16
    )
    key_rows = rotate(projected[:, :, 1] + key_full, cosine_table, sine_table, 1.0).astype(
        jnp.bfloat16
    )
    values = (projected[:, :, 2] + qv_wide[1]).astype(jnp.bfloat16)
    placeholder = jnp.zeros((), jnp.float32)
    group_inputs = (to_groups(queries), to_groups(key_rows), to_groups(values), to_groups(allowed))
    unused, (mixed_groups, log_groups) = lax.scan(attend_group, placeholder, group_inputs)
    mixed_rows = mixed_groups.reshape(row_count, local_width)
    hidden = jnp.dot(normed_low, up_all, preferred_element_type=jnp.float32) + up_shift_all.reshape(
        -1
    ).astype(jnp.float32)
    activated = gelu_tanh(hidden).astype(jnp.bfloat16)
    branches = jnp.dot(mixed_rows, dense_all, preferred_element_type=jnp.float32) + jnp.dot(
        activated, down_all, preferred_element_type=jnp.float32
    )
    dense_shift = dense_shift_all.astype(jnp.float32)
    down_shift = down_shift_all.astype(jnp.float32)
    summed_out = lax.psum(branches, "tensor")
    block_output = (widened + summed_out + dense_shift + down_shift).astype(jnp.bfloat16)
    gain_back, qkv_back, dense_back, up_back, down_back = (
        lax.all_gather(norm_gain, "dp", axis=0, tiled=True),
        lax.all_gather(qkv_weight, "dp", axis=0, tiled=True),
        lax.all_gather(dense_weight, "dp", axis=1, tiled=True),
        lax.all_gather(up_weight, "dp", axis=0, tiled=True),
        lax.all_gather(down_weight, "dp", axis=1, tiled=True),
    )
    grad_wide = cotangent.astype(jnp.float32)
    grad_bias_out = jnp.sum(grad_wide, axis=0)
    grad_dense = jnp.dot(mixed_rows.T, cotangent, preferred_element_type=jnp.float32)
    grad_down = jnp.dot(activated.T, cotangent, preferred_element_type=jnp.float32)
    grad_mixed = (
        jnp.dot(cotangent, dense_back.T, preferred_element_type=jnp.float32)
        .astype(jnp.bfloat16)
        .reshape(seqs_here, SEQ, heads_here, HEAD)
    )
    grad_act = jnp.dot(cotangent, down_back.T, preferred_element_type=jnp.float32)
    grad_hidden = jax.vjp(gelu_tanh, hidden)[1](grad_act)[0]
    grad_up_bias = jnp.sum(grad_hidden, axis=0).reshape(up_shift_all.shape)
    grad_hidden_low = grad_hidden.astype(jnp.bfloat16)
    grad_up = jnp.dot(normed_low.T, grad_hidden_low, preferred_element_type=jnp.float32)
    back_inputs = group_inputs + (log_groups, to_groups(grad_mixed))
    unused_back, (query_groups, key_groups, value_groups) = lax.scan(
        attend_back_group, placeholder, back_inputs
    )
    grad_queries = rotate(from_groups(query_groups), cosine_table, sine_table, -1.0)
    grad_keys = rotate(from_groups(key_groups), cosine_table, sine_table, -1.0)
    grad_values = from_groups(value_groups)
    grad_qv = jnp.stack([jnp.sum(grad_queries, axis=(0, 1)), jnp.sum(grad_values, axis=(0, 1))])
    grad_key_bias = jnp.sum(grad_keys[..., :ROT], axis=(0, 1))
    grad_projected = (
        jnp.stack([grad_queries, grad_keys, grad_values], axis=2)
        .reshape(row_count, 3 * local_width)
        .astype(jnp.bfloat16)
    )
    grad_qkv = jnp.dot(normed_low.T, grad_projected, preferred_element_type=jnp.float32).reshape(
        model_width, 3, local_width
    )
    grad_normed_part = jnp.dot(
        grad_projected,
        qkv_back.reshape(model_width, 3 * local_width).T,
        preferred_element_type=jnp.float32,
    ) + jnp.dot(grad_hidden_low, up_back.T, preferred_element_type=jnp.float32)
    grad_normed = lax.psum(grad_normed_part.astype(jnp.bfloat16), "tensor").astype(jnp.float32)
    grad_gain = jnp.sum(grad_normed * normed, axis=0)
    grad_shift = jnp.sum(grad_normed, axis=0)
    scaled = grad_normed * gain_back.astype(jnp.float32)
    input_grad = (
        inv_std
        * (
            scaled
            - jnp.mean(scaled, axis=1, keepdims=True)
            - normed * jnp.mean(scaled * normed, axis=1, keepdims=True)
        )
        + grad_wide
    )
    summed = (
        lax.psum_scatter(grad_gain, "dp", scatter_dimension=0, tiled=True),
        lax.psum_scatter(grad_shift, "dp", scatter_dimension=0, tiled=True),
        lax.psum_scatter(grad_qkv, "dp", scatter_dimension=0, tiled=True),
        lax.psum_scatter(grad_qv, "dp", scatter_dimension=2, tiled=True),
        lax.psum_scatter(grad_key_bias, "dp", scatter_dimension=1, tiled=True),
        lax.psum_scatter(grad_dense, "dp", scatter_dimension=1, tiled=True),
        lax.psum_scatter(grad_bias_out, "dp", scatter_dimension=0, tiled=True),
        lax.psum_scatter(grad_up, "dp", scatter_dimension=0, tiled=True),
        lax.psum_scatter(grad_up_bias, "dp", scatter_dimension=1, tiled=True),
        lax.psum_scatter(grad_down, "dp", scatter_dimension=1, tiled=True),
    )
    return (
        block_output,
        input_grad,
        summed[0],
        summed[1],
        summed[2],
        summed[3],
        summed[4],
        summed[5],
        summed[6],
        summed[7],
        summed[8],
        summed[9],
        summed[6],
    )


def solution(mesh):
    in_specs = (
        P("dp", None),
        P("dp"),
        P("dp"),
        P("dp"),
        P("dp", None, "tensor"),
        P(None, "tensor", "dp"),
        P("tensor", "dp"),
        P("tensor", "dp"),
        P("dp"),
        P("dp", "tensor"),
        P("tensor", "dp"),
        P("tensor", "dp"),
        P("dp"),
        P("dp", None),
    )
    out_specs = (
        P("dp", None),
        P("dp", None),
        P("dp"),
        P("dp"),
        P("dp", None, "tensor"),
        P(None, "tensor", "dp"),
        P("tensor", "dp"),
        P("tensor", "dp"),
        P("dp"),
        P("dp", "tensor"),
        P("tensor", "dp"),
        P("tensor", "dp"),
        P("dp"),
    )
    return jax.shard_map(local, mesh=mesh, in_specs=in_specs, out_specs=out_specs, check_vma=False)
```

profile of v0, /device:TPU:0, one launch (start us, length us, event | category | flops | bytes accessed | tf_op | source)
XLA Modules:
  0.0 1116.1 jit_solution(14657728340286387230)
XLA Ops:
  22.3 10.4 all-gather.1
  32.7 9.1 all-gather
  41.8 8.0 all-gather.2
  49.8 9.2 all_gather.45
  59.8 8.6 all_gather.41
  74.7 6.2 convolution_convert_fusion
  89.3 10.1 fusion.146
  101.6 13.5 %while.26 = (s32[]{:T(128)}, bf16[2,1,512,8,64]{2,4,3,1,0:T(8,128)(2,1)}, f32[2,1,8,512,1]{3,2,4,1,0:T(8,128)S(1)}, bf16[2,1,512,8,64]{2,4,3,1,0:T(8,128)(2,1)},...) while((s32[]{:T(128)}, ...), condition=%wide.region_7.8_spmd, body=%wide.region_4.7_spmd.sunk | while | flops 560197632 | bytes 41289912 | solution.py:185
  115.0 85.6 %while.27 = (s32[]{:T(128)}, f32[2,1,512,8,64]{2,4,3,1,0:T(8,128)}, f32[2,1,512,8,64]{2,4,3,1,0:T(8,128)}, f32[2,1,512,8,64]{2,4,3,1,0:T(8,128)}, bf16[2,1,512,8...) while((s32[]{:T(128)}, f32[2,1,512,8,64]{2,4,3,1,0:T(8,128)}, ...), condition=%wide.region_11.12_spmd, body=%wide.region_9.11_spmd.sunk | while | flops 1396712448 | bytes 159765776 | solution.py:220
  128.5 14.5 %fusion.204 = f32[2,1,512,8,64]{2,4,3,1,0:T(8,128)} fusion(f32[2,1,512,8,64]{2,4,3,1,0:T(8,128)} %get-tuple-element.472, s32[]{:T(128)S(6)} %copy.169, f32[8,512,512]{1,2,0:T(8,128)} %fusion.201, f32[8,512,512]{1,2,0:T(8,128)} %copy-done, f32[8,512]{1,0:T(8,128)S(1)} %dynamic-slice_bitcast_fusion.7, ...), kind=kOutput, calls=%fused_computation.46.clone.1 | convolution fusion | flops 291508736 | bytes 35685376 | tf_op jit(solution)/shard_map/while/body/eval_jaxpr/nhqk,nqhd->nkhd/dot_general | solution.py:95
  143.0 14.4 %fusion.203 = f32[2,1,512,8,64]{2,4,3,1,0:T(8,128)} fusion(f32[2,1,512,8,64]{2,4,3,1,0:T(8,128)} %get-tuple-element.471, s32[]{:T(128)S(6)} %copy.169, f32[8,512,512]{1,2,0:T(8,128)} %fusion.201, f32[8,512,512]{1,2,0:T(8,128)} %copy-done, f32[8,512]{1,0:T(8,128)S(1)} %dynamic-slice_bitcast_fusion.7, ...), kind=kOutput, calls=%fused_computation.44.clone.1 | convolution fusion | flops 291508736 | bytes 35685376 | tf_op jit(solution)/shard_map/while/body/eval_jaxpr/nhqk,nkhd->nqhd/dot_general | solution.py:92
  170.4 15.7 %fusion.204 = f32[2,1,512,8,64]{2,4,3,1,0:T(8,128)} fusion(f32[2,1,512,8,64]{2,4,3,1,0:T(8,128)} %get-tuple-element.472, s32[]{:T(128)S(6)} %copy.169, f32[8,512,512]{1,2,0:T(8,128)} %fusion.201, f32[8,512,512]{1,2,0:T(8,128)} %copy-done, f32[8,512]{1,0:T(8,128)S(1)} %dynamic-slice_bitcast_fusion.7, ...), kind=kOutput, calls=%fused_computation.46.clone.1 | convolution fusion | flops 291508736 | bytes 35685376 | tf_op jit(solution)/shard_map/while/body/eval_jaxpr/nhqk,nqhd->nkhd/dot_general | solution.py:95
  186.0 14.4 %fusion.203 = f32[2,1,512,8,64]{2,4,3,1,0:T(8,128)} fusion(f32[2,1,512,8,64]{2,4,3,1,0:T(8,128)} %get-tuple-element.471, s32[]{:T(128)S(6)} %copy.169, f32[8,512,512]{1,2,0:T(8,128)} %fusion.201, f32[8,512,512]{1,2,0:T(8,128)} %copy-done, f32[8,512]{1,0:T(8,128)S(1)} %dynamic-slice_bitcast_fusion.7, ...), kind=kOutput, calls=%fused_computation.44.clone.1 | convolution fusion | flops 291508736 | bytes 35685376 | tf_op jit(solution)/shard_map/while/body/eval_jaxpr/nhqk,nkhd->nqhd/dot_general | solution.py:92
  211.5 15.6 %fusion.147 = f32[1024,2048]{1,0:T(8,128)} fusion(bf16[1024,2048]{1,0:T(8,128)(2,1)} %fusion.106, bf16[2048,2048]{1,0:T(8,128)(2,1)} %all-gather.14.cloned.1.call-done), kind=kOutput, calls=%fused_computation.179 | convolution fusion | flops 8589934592 | bytes 20971520 | tf_op jit(solution)/shard_map/dot_general | solution.py:187
  227.1 19.2 %fusion.143 = (f32[2048]{0:T(1024)S(1)}, bf16[1024,2048]{1,0:T(8,128)(2,1)S(1)}) fusion(f32[1024,2048]{1,0:T(8,128)} %fusion.147, f32[2048]{0:T(1024)S(1)} %copy-done.25, bf16[1024,2048]{1,0:T(8,128)(2,1)} %param.31, bf16[2048,2048]{1,0:T(8,128)(2,1)} %all-gather.16.cloned.1.call-done), kind=kOutput, calls=%fused_computation.176 | convolution fusion | flops 8636069888 | bytes 25182208 | tf_op jit(solution)/shard_map/dot_general | solution.py:214
  246.4 11.1 fusion.129
  257.4 12.7 %add_convert_fusion = bf16[1024,2048]{1,0:T(8,128)(2,1)} fusion(f32[1024,2048]{1,0:T(8,128)} %fusion.129, bf16[1024,1536]{0,1:T(8,128)(2,1)S(1)} %bitcast.234, bf16[2048,1536]{0,1:T(8,128)(2,1)} %bitcast.255), kind=kOutput, calls=%fused_computation.111 | convolution fusion | flops 6446645248 | bytes 22020096 | tf_op jit(solution)/shard_map/dot_general | solution.py:236
  272.7 16.4 %fusion.142 = f32[1024,2048]{1,0:T(8,128)S(1)} fusion(bf16[2048,2048]{1,0:T(8,128)(2,1)} %all-gather.16.cloned.1.call-done, f32[1024,2048]{1,0:T(8,128)} %fusion.147, f32[2048]{0:T(1024)S(1)} %copy-done.25), kind=kOutput, calls=%fused_computation.175 | convolution fusion | flops 8610906112 | bytes 25174016 | tf_op jit(solution)/shard_map/dot_general | solution.py:191
  295.0 6.5 fusion.148
  301.6 12.7 %fusion.121 = f32[2048,3,512]{2,0,1:T(8,128)} fusion(bf16[3,512,1024]{2,1,0:T(8,128)(2,1)} %bitcast.235, bf16[1024,2048]{1,0:T(8,128)(2,1)} %fusion.106), kind=kOutput, calls=%fused_computation.114 | convolution fusion | flops 6442450944 | bytes 19922944 | tf_op jit(solution)/shard_map/dot_general | solution.py:233
  314.3 17.3 %fusion.141 = f32[2048,2048]{1,0:T(8,128)} fusion(bf16[1024,2048]{1,0:T(8,128)(2,1)} %param.31, f32[1024,2048]{1,0:T(8,128)} %fusion.147, f32[2048]{0:T(1024)S(1)} %copy-done.25), kind=kOutput, calls=%fused_computation.174 | convolution fusion | flops 8610906112 | bytes 29368320 | tf_op jit(solution)/shard_map/dot_general | solution.py:208
  331.9 15.2 %fusion.127 = f32[2048,2048]{1,0:T(8,128)} fusion(bf16[1024,2048]{1,0:T(8,128)(2,1)} %fusion.106, bf16[1024,2048]{1,0:T(8,128)(2,1)} %copy-done.33), kind=kOutput, calls=%fused_computation.126 | convolution fusion | flops 8589934592 | bytes 25165824 | tf_op jit(solution)/shard_map/dot_general | solution.py:218
  350.3 8.6 all-gather.4
  358.9 8.3 all-gather.3
  370.3 54.7 %all-reduce.14.cloned.1.call-done = bf16[1024,2048]{1,0:T(8,128)(2,1)} async-done(((bf16[1024,2048]{1,0:T(8,128)(2,1)}), bf16[1024,2048]{1,0:T(8,128)(2,1)}) %all-reduce.14.cloned.1.call-update) | async-done | bytes 4194320 | tf_op jit(solution)/shard_map/psum | solution.py:241
  431.2 285.9 %all-reduce.12.cloned.1.call-done = f32[1024,2048]{1,0:T(8,128)} async-done(((f32[1024,2048]{1,0:T(8,128)}), f32[1024,2048]{1,0:T(8,128)}) %all-reduce.12.cloned.1.call-update) | async-done | bytes 8388624 | tf_op jit(solution)/shard_map/psum | solution.py:196
  717.2 13.4 %convert_reduce_fusion.2 = (f32[2048]{0:T(1024)S(1)}, f32[1024,2048]{1,0:T(8,128)}, bf16[1024,2048]{1,0:T(8,128)(2,1)}) fusion(bf16[1024,2048]{1,0:T(8,128)(2,1)} %param.31, f32[1024]{0:T(1024)S(1)} %broadcast_multiply_fusion.1, f32[1024]{0:T(1024)S(1)} %copy-done.22, bf16[1024,2048]{1,0:T(8,128)(2,1)} %param.18, f32[1024]{0:T(1024)S(1)} %broadcast_multiply_fusion.2, ...), kind=kLoop, calls=%fused_computation.89 | loop fusion | flops 33552384 | bytes 33603584 | tf_op jit(solution)/shard_map/reduce_sum | solution.py:206
  730.6 25.7 %all-reduce.8 = (f32[2048]{0:T(1024)S(1)}, f32[2048]{0:T(1024)S(1)}, f32[2,8,64]{2,1,0:T(8,128)S(1)}, f32[8,32]{0,1:T(8,128)S(1)}, f32[2048]{0:T(1024)S(1)}, /*index=5*/f32[32,64]{1,0:T(8,128)S(1)}) all-reduce(f32[2048]{0:T(1024)S(1)} %get-tuple-element.247, ...), channel_id=2, replica_groups=mesh['dp'=8,'tensor'=4] {'dp'}, use_global_device_ids=true, to_apply=%region_16.17.clone | all-reduce | flops 9472 | bytes 75776
  759.6 12.1 %reduce-scatter.9.cloned.1.call-done = f32[512,256]{1,0:T(8,128)} async-done(((f32[512,2048]{1,0:T(8,128)}), f32[512,256]{1,0:T(8,128)}) %reduce-scatter.9.cloned.1.call-update) | async-done | bytes 524304 | tf_op jit(solution)/shard_map/reduce_scatter | solution.py:260
  771.7 96.2 %reduce-scatter.7.cloned.1.call-done = f32[256,3,512]{2,0,1:T(8,128)} async-done(((f32[2048,3,512]{2,0,1:T(8,128)}), f32[256,3,512]{2,0,1:T(8,128)}) %reduce-scatter.7.cloned.1.call-update) | async-done | bytes 1572880 | tf_op jit(solution)/shard_map/reduce_scatter | solution.py:257
  867.9 120.1 %reduce-scatter.13.cloned.1.call-done = f32[2048,256]{1,0:T(8,128)} async-done(((f32[2048,2048]{1,0:T(8,128)}), f32[2048,256]{1,0:T(8,128)}) %reduce-scatter.13.cloned.1.call-update) | async-done | bytes 2097168 | tf_op jit(solution)/shard_map/reduce_scatter | solution.py:264
  988.0 120.2 %reduce-scatter.11.cloned.1.call-done = f32[256,2048]{1,0:T(8,128)} async-done(((f32[2048,2048]{1,0:T(8,128)}), f32[256,2048]{1,0:T(8,128)}) %reduce-scatter.11.cloned.1.call-update) | async-done | bytes 2097168 | tf_op jit(solution)/shard_map/reduce_scatter | solution.py:262
  (205 shorter events, 106.2 us)
Async XLA Ops:
  7.2 34.6 %copy-start.28 = (bf16[8,4]{0,1:T(4,128)(2,1)S(1)}, bf16[8,4]{0,1:T(4,128)(2,1)}, u32[]{:S(2)}) copy-start(bf16[8,4]{0,1:T(4,128)(2,1)} %param.24) | copy-start | bytes 196
  7.2 42.6 %copy-start.27 = (bf16[32,8]{0,1:T(8,128)(2,1)S(1)}, bf16[32,8]{0,1:T(8,128)(2,1)}, u32[]{:S(2)}) copy-start(bf16[32,8]{0,1:T(8,128)(2,1)} %param.28) | copy-start | bytes 1540
  7.2 67.5 %all-gather.12.cloned.1.call-start = ((), (), s32[]{:S(2)}) async-start(), calls=%async_computation.5 | async-start | bytes 2359296 | tf_op jit(solution)/shard_map/all_gather | solution.py:123
  7.9 81.4 %all-gather.10.cloned.1.call-start = ((), (), s32[]{:S(2)}) async-start(), calls=%async_computation.4 | async-start | bytes 7077888 | tf_op jit(solution)/shard_map/all_gather | solution.py:120
  10.3 201.2 %all-gather.14.cloned.1.call-start = ((), (), s32[]{:S(2)}) async-start(), calls=%async_computation.6 | async-start | bytes 9437184 | tf_op jit(solution)/shard_map/all_gather | solution.py:125
  11.0 216.1 %all-gather.16.cloned.1.call-start = ((), (), s32[]{:S(2)}) async-start(), calls=%async_computation.7 | async-start | bytes 9437184 | tf_op jit(solution)/shard_map/all_gather | solution.py:127
  11.6 413.4 %all-reduce.14.cloned.1.call-start = ((), (), s32[]{:S(2)}) async-start(), calls=%async_computation.9 | async-start | bytes 8388608 | tf_op jit(solution)/shard_map/psum | solution.py:241
  18.7 62.2 %copy-start.21 = (f32[1024]{0:T(1024)}, f32[1024]{0:T(1024)S(1)}, u32[]{:S(2)}) copy-start(f32[1024]{0:T(1024)S(1)} %broadcast_multiply_fusion.3) | copy-start | bytes 12292
  22.2 58.6 %copy-start.23 = (f32[1024]{0:T(1024)}, f32[1024]{0:T(1024)S(1)}, u32[]{:S(2)}) copy-start(f32[1024]{0:T(1024)S(1)} %add_rsqrt_fusion) | copy-start | bytes 12292
  41.7 39.1 %copy-start.19 = (f32[8,1,256]{2,1,0:T(1,128)}, f32[8,1,256]{2,1,0:T(1,128)S(1)}, u32[]{:S(2)}) copy-start(f32[8,1,256]{2,1,0:T(1,128)S(1)} %convert_element_type.142) | copy-start | bytes 24580
  115.0 88.3 %copy-start.18 = (f32[2,512,16]{1,2,0:T(8,128)S(1)}, f32[2,512,16]{1,2,0:T(8,128)}, u32[]{:S(2)}) copy-start(f32[2,512,16]{1,2,0:T(8,128)} %get-tuple-element.316) | copy-start | bytes 196612
  115.0 5.1 copy-start.1
  115.0 5.1 copy-start.6
  115.1 8.7 copy-start.3
  157.5 8.2 copy-start.3
  200.6 6.3 copy-start.8
  211.5 45.9 %copy-start.14 = (bf16[192,8,2,512]{3,1,2,0:T(8,128)(2,1)}, bf16[192,8,2,512]{3,1,2,0:T(8,128)(2,1)S(1)}, u32[]{:S(2)}) copy-start(bf16[192,8,2,512]{3,1,2,0:T(8,128)(2,1)S(1)} %copy.149) | copy-start | bytes 9437188
  211.5 15.6 %copy-start.25 = (f32[2048]{0:T(1024)S(1)}, f32[2048]{0:T(1024)}, u32[]{:S(2)}) copy-start(f32[2048]{0:T(1024)} %reshape.385) | copy-start | bytes 24580
  227.1 19.2 %copy-start.29 = (bf16[2048,2048]{1,0:T(8,128)(2,1)S(1)}, bf16[2048,2048]{1,0:T(8,128)(2,1)}, u32[]{:S(2)}) copy-start(bf16[2048,2048]{1,0:T(8,128)(2,1)} %all-gather.14.cloned.1.call-done) | copy-start | bytes 25165828
  246.3 11.1 copy-start.33
  270.1 447.1 %all-reduce.12.cloned.1.call-start = ((), (), s32[]{:S(2)}) async-start(), calls=%async_computation.8 | async-start | bytes 16777216 | tf_op jit(solution)/shard_map/psum | solution.py:196
  272.7 16.4 %copy-start.15 = (bf16[512,2048]{1,0:T(8,128)(2,1)S(1)}, bf16[512,2048]{1,0:T(8,128)(2,1)}, u32[]{:S(2)}) copy-start(bf16[512,2048]{1,0:T(8,128)(2,1)} %all-gather.12.cloned.1.call-done) | copy-start | bytes 6291460
  294.8 476.9 %reduce-scatter.9.cloned.1.call-start = ((), (), s32[]{:S(2)}) async-start(), calls=%async_computation.11 | async-start | bytes 4718592 | tf_op jit(solution)/shard_map/reduce_scatter | solution.py:260
  301.5 566.4 %reduce-scatter.7.cloned.1.call-start = ((), (), s32[]{:S(2)}) async-start(), calls=%async_computation.10 | async-start | bytes 14155776 | tf_op jit(solution)/shard_map/reduce_scatter | solution.py:257
  314.2 673.8 %reduce-scatter.13.cloned.1.call-start = ((), (), s32[]{:S(2)}) async-start(), calls=%async_computation.13 | async-start | bytes 18874368 | tf_op jit(solution)/shard_map/reduce_scatter | solution.py:264
  331.6 776.7 %reduce-scatter.11.cloned.1.call-start = ((), (), s32[]{:S(2)}) async-start(), calls=%async_computation.12 | async-start | bytes 18874368 | tf_op jit(solution)/shard_map/reduce_scatter | solution.py:262
  347.1 20.1 %copy-start.9 = (f32[2,1,512,8,64]{2,4,3,1,0:T(8,128)S(1)}, f32[2,1,512,8,64]{2,4,3,1,0:T(8,128)}, u32[]{:S(2)}) copy-start(f32[2,1,512,8,64]{2,4,3,1,0:T(8,128)} %get-tuple-element.109) | copy-start | bytes 6291460
  347.1 21.7 %copy-start.5 = (f32[2,512,8,32]{1,3,2,0:T(8,128)S(1)}, f32[2,512,8,32]{1,3,2,0:T(8,128)}, u32[]{:S(2)}) copy-start(f32[2,512,8,32]{1,3,2,0:T(8,128)} %copy-done.4) | copy-start | bytes 3145732
  347.1 77.9 %copy-start.20 = (f32[8,1,256]{2,1,0:T(1,128)S(1)}, f32[8,1,256]{2,1,0:T(1,128)}, u32[]{:S(2)}) copy-start(f32[8,1,256]{2,1,0:T(1,128)} %copy-done.19) | copy-start | bytes 24580
  347.1 77.9 %copy-start.22 = (f32[1024]{0:T(1024)S(1)}, f32[1024]{0:T(1024)}, u32[]{:S(2)}) copy-start(f32[1024]{0:T(1024)} %copy-done.21) | copy-start | bytes 12292
  347.1 77.9 %copy-start.24 = (f32[1024]{0:T(1024)S(1)}, f32[1024]{0:T(1024)}, u32[]{:S(2)}) copy-start(f32[1024]{0:T(1024)} %copy-done.23) | copy-start | bytes 12292
  757.0 351.8 %copy-start.26 = (f32[256]{0:T(256)}, f32[256]{0:T(256)S(1)}, u32[]{:S(2)}) copy-start(f32[256]{0:T(256)S(1)} %dynamic-slice.9) | copy-start | bytes 3076
  (20 other events, 47.7 us)
Sparse Core Ops, SparseCore 0:
  9.9 30.8 all-gather.11
  42.6 46.6 all-gather.9
  91.2 54.2 all-gather.13
  147.2 55.8 all-gather.15
  270.2 154.7 all-reduce.13
  427.3 289.7 all-reduce.11
  721.1 50.5 reduce-scatter.8
  775.7 92.0 reduce-scatter.6
  872.0 115.9 reduce-scatter.12
  992.0 116.2 reduce-scatter.10
where the time goes:
time: 1120 us
  waiting for transfers between devices  695 us (62%)
  matrix products  232 us (21%)
  blocking collectives  87.8 us (8%)
  other arithmetic  44.5 us (4%)
  local copies, waits for them, and re-layouts  39 us (3%)
  between operations  17.1 us (2%)
    psum x1, waiting for transfers between devices, local(): summed_out = lax.psum(branches, 'tensor')  286 us
    reduce_scatter x1, waiting for transfers between devices, local(): lax.psum_scatter(grad_up, 'dp', scatter_dimension=0, tiled=True)  120 us
    reduce_scatter x1, waiting for transfers between devices, local(): lax.psum_scatter(grad_down, 'dp', scatter_dimension=1, tiled=True)  120 us
    reduce_scatter x1, waiting for transfers between devices, local(): lax.psum_scatter(grad_qkv, 'dp', scatter_dimension=0, tiled=True)  96.2 us
    psum x1, waiting for transfers between devices, local(): lax.psum(grad_normed_part.astype(jnp.bfloat16), 'tensor')  54.7 us
    dot_general x2, matrix products, attend_back_group(): jnp.einsum('nhqk,nqhd->nkhd', grad_scores, queries, preferred_element_typ...  30.2 us
    dot_general x2, matrix products, attend_back_group(): jnp.einsum('nhqk,nkhd->nqhd', grad_scores, key_rows, preferred_element_ty...  28.8 us
    unnamed x1, blocking collectives  25.7 us
  transfers between devices with their start and end apart: 10, of which 7 were waited for; matrix products, arithmetic and copies ran while one was open for 23% of the time, Pallas kernels for 0%

commit v1 on v0

--- a/solution.py
+++ b/solution.py
@@ -193,7 +193,11 @@
     )
     dense_shift = dense_shift_all.astype(jnp.float32)
     down_shift = down_shift_all.astype(jnp.float32)
-    summed_out = lax.psum(branches, "tensor")
+    summed_out = branches
+    for hop in (1, 2):
+        summed_out = summed_out + lax.ppermute(
+            summed_out, "tensor", [(dev, dev ^ hop) for dev in range(4)]
+        )
     block_output = (widened + summed_out + dense_shift + down_shift).astype(jnp.bfloat16)
     gain_back, qkv_back, dense_back, up_back, down_back = (
         lax.all_gather(norm_gain, "dp", axis=0, tiled=True),

time: 1120 us -> 1020 us (0.911)
  waiting for transfers between devices: 695 us -> 586 us
  other arithmetic: 44.5 us -> 59.1 us
    ppermute x0 -> x2, waiting for transfers between devices: none -> 580 us  [local(): lax.ppermute(summed_out, 'tensor', [(dev, dev ^ hop) for dev in range(4)])]
    psum x1 -> x0, waiting for transfers between devices: 286 us -> none  [local(): summed_out = lax.psum(branches, 'tensor')]
    reduce_scatter x1, waiting for transfers between devices: 120 us -> 0.01 us  [local(): lax.psum_scatter(grad_up, 'dp', scatter_dimension=0, tiled=True)]
    reduce_scatter x1, waiting for transfers between devices: 120 us -> 0.01 us  [local(): lax.psum_scatter(grad_down, 'dp', scatter_dimension=1, tiled=True)]
    reduce_scatter x1, waiting for transfers between devices: 96.2 us -> 0.01 us  [local(): lax.psum_scatter(grad_qkv, 'dp', scatter_dimension=0, tiled=True)]
    psum x1, waiting for transfers between devices: 54.7 us -> 0.01 us  [local(): lax.psum(grad_normed_part.astype(jnp.bfloat16), 'tensor')]
    add x0 -> x1, other arithmetic: none -> 12.3 us  [local(): summed_out + lax.ppermute(summed_out, 'tensor', [(dev, dev ^ hop) for dev...]
    reduce_scatter x1, waiting for transfers between devices: 12.1 us -> 0.01 us  [local(): lax.psum_scatter(grad_dense, 'dp', scatter_dimension=1, tiled=True)]
  transfers between devices with their start and end apart: 10 -> 11, of which waited for: 7 -> 3; matrix products, arithmetic and copies ran while one was open for 23% -> 26% of each run, Pallas kernels for 0% -> 0%
where the time goes in v1:
time: 1020 us
  waiting for transfers between devices  586 us (57%)
  matrix products  228 us (22%)
  blocking collectives  84.9 us (8%)
  other arithmetic  59.1 us (6%)
  local copies, waits for them, and re-layouts  41.8 us (4%)
  between operations  16.6 us (2%)
    ppermute x2, waiting for transfers between devices, local(): lax.ppermute(summed_out, 'tensor', [(dev, dev ^ hop) for dev in range(4)])  580 us
    dot_general x2, matrix products, attend_back_group(): jnp.einsum('nhqk,nqhd->nkhd', grad_scores, queries, preferred_element_typ...  30.2 us
    dot_general x2, matrix products, attend_back_group(): jnp.einsum('nhqk,nkhd->nqhd', grad_scores, key_rows, preferred_element_ty...  28.8 us
    unnamed x1, blocking collectives  22.9 us
  transfers between devices with their start and end apart: 11, of which 3 were waited for; matrix products, arithmetic and copies ran while one was open for 26% of the time, Pallas kernels for 0%

profile of v1, /device:TPU:0, one launch (start us, length us, event | category | flops | bytes accessed | tf_op | source)
XLA Modules:
  0.0 1020.9 jit_solution(14425690304880803611)
XLA Ops:
  22.3 10.4 %all-gather.1 = bf16[8,1,256]{2,1,0:T(2,128)(2,1)S(1)} all-gather(bf16[1,1,256]{2,1,0:T(2,128)(2,1)S(1)} %reshape.388), channel_id=1, replica_groups=mesh['dp'=8,'tensor'=4] {'dp'}, dimensions={0}, use_global_device_ids=true | all-gather | bytes 4608 | tf_op jit(solution)/shard_map/all_gather | solution.py:119
  32.8 9.1 all-gather
  41.8 8.0 all-gather.2
  49.9 9.2 all_gather.45
  59.9 8.3 all_gather.41
  69.7 4.7 fusion.106
  74.4 6.2 convolution_convert_fusion
  89.3 10.1 fusion.146
  101.5 13.5 %while.26 = (s32[]{:T(128)}, bf16[2,1,512,8,64]{2,4,3,1,0:T(8,128)(2,1)}, f32[2,1,8,512,1]{3,2,4,1,0:T(8,128)S(1)}, bf16[2,1,512,8,64]{2,4,3,1,0:T(8,128)(2,1)},...) while((s32[]{:T(128)}, ...), condition=%wide.region_7.8_spmd, body=%wide.region_4.7_spmd.sunk | while | flops 560197632 | bytes 41289912 | solution.py:185
  115.0 85.7 %while.27 = (s32[]{:T(128)}, f32[2,1,512,8,64]{2,4,3,1,0:T(8,128)}, f32[2,1,512,8,64]{2,4,3,1,0:T(8,128)}, f32[2,1,512,8,64]{2,4,3,1,0:T(8,128)}, bf16[2,1,512,8...) while((s32[]{:T(128)}, f32[2,1,512,8,64]{2,4,3,1,0:T(8,128)}, ...), condition=%wide.region_10.11_spmd, body=%wide.region_8.10_spmd.sunk | while | flops 1396712448 | bytes 159765776 | solution.py:224
  128.5 14.5 %fusion.204 = f32[2,1,512,8,64]{2,4,3,1,0:T(8,128)} fusion(f32[2,1,512,8,64]{2,4,3,1,0:T(8,128)} %get-tuple-element.472, s32[]{:T(128)S(6)} %copy.169, f32[8,512,512]{1,2,0:T(8,128)} %fusion.201, f32[8,512,512]{1,2,0:T(8,128)} %copy-done, f32[8,512]{1,0:T(8,128)S(1)} %dynamic-slice_bitcast_fusion.7, ...), kind=kOutput, calls=%fused_computation.46.clone.1 | convolution fusion | flops 291508736 | bytes 35685376 | tf_op jit(solution)/shard_map/while/body/eval_jaxpr/nhqk,nqhd->nkhd/dot_general | solution.py:95
  143.0 14.4 %fusion.203 = f32[2,1,512,8,64]{2,4,3,1,0:T(8,128)} fusion(f32[2,1,512,8,64]{2,4,3,1,0:T(8,128)} %get-tuple-element.471, s32[]{:T(128)S(6)} %copy.169, f32[8,512,512]{1,2,0:T(8,128)} %fusion.201, f32[8,512,512]{1,2,0:T(8,128)} %copy-done, f32[8,512]{1,0:T(8,128)S(1)} %dynamic-slice_bitcast_fusion.7, ...), kind=kOutput, calls=%fused_computation.44.clone.1 | convolution fusion | flops 291508736 | bytes 35685376 | tf_op jit(solution)/shard_map/while/body/eval_jaxpr/nhqk,nkhd->nqhd/dot_general | solution.py:92
  165.6 4.7 fusion.201
  170.3 15.7 %fusion.204 = f32[2,1,512,8,64]{2,4,3,1,0:T(8,128)} fusion(f32[2,1,512,8,64]{2,4,3,1,0:T(8,128)} %get-tuple-element.472, s32[]{:T(128)S(6)} %copy.169, f32[8,512,512]{1,2,0:T(8,128)} %fusion.201, f32[8,512,512]{1,2,0:T(8,128)} %copy-done, f32[8,512]{1,0:T(8,128)S(1)} %dynamic-slice_bitcast_fusion.7, ...), kind=kOutput, calls=%fused_computation.46.clone.1 | convolution fusion | flops 291508736 | bytes 35685376 | tf_op jit(solution)/shard_map/while/body/eval_jaxpr/nhqk,nqhd->nkhd/dot_general | solution.py:95
  186.0 14.4 %fusion.203 = f32[2,1,512,8,64]{2,4,3,1,0:T(8,128)} fusion(f32[2,1,512,8,64]{2,4,3,1,0:T(8,128)} %get-tuple-element.471, s32[]{:T(128)S(6)} %copy.169, f32[8,512,512]{1,2,0:T(8,128)} %fusion.201, f32[8,512,512]{1,2,0:T(8,128)} %copy-done, f32[8,512]{1,0:T(8,128)S(1)} %dynamic-slice_bitcast_fusion.7, ...), kind=kOutput, calls=%fused_computation.44.clone.1 | convolution fusion | flops 291508736 | bytes 35685376 | tf_op jit(solution)/shard_map/while/body/eval_jaxpr/nhqk,nkhd->nqhd/dot_general | solution.py:92
  211.7 15.6 %fusion.147 = f32[1024,2048]{1,0:T(8,128)} fusion(bf16[1024,2048]{1,0:T(8,128)(2,1)} %fusion.106, bf16[2048,2048]{1,0:T(8,128)(2,1)} %all-gather.14.cloned.1.call-done), kind=kOutput, calls=%fused_computation.179 | convolution fusion | flops 8589934592 | bytes 20971520 | tf_op jit(solution)/shard_map/dot_general | solution.py:187
  227.2 18.9 %fusion.143 = (f32[2048]{0:T(1024)S(1)}, bf16[1024,2048]{1,0:T(8,128)(2,1)S(1)}) fusion(f32[1024,2048]{1,0:T(8,128)} %fusion.147, f32[2048]{0:T(1024)S(1)} %copy-done.28, bf16[1024,2048]{1,0:T(8,128)(2,1)} %param.31, bf16[2048,2048]{1,0:T(8,128)(2,1)} %all-gather.16.cloned.1.call-done), kind=kOutput, calls=%fused_computation.176 | convolution fusion | flops 8636069888 | bytes 25182208 | tf_op jit(solution)/shard_map/dot_general | solution.py:218
  246.2 11.2 %fusion.129 = f32[1024,2048]{1,0:T(8,128)} fusion(bf16[2048,2048]{1,0:T(8,128)(2,1)S(1)} %copy-done.32, bf16[1024,2048]{1,0:T(8,128)(2,1)S(1)} %get-tuple-element.294), kind=kOutput, calls=%fused_computation.128 | convolution fusion | flops 8589934592 | bytes 20971520 | tf_op jit(solution)/shard_map/dot_general | solution.py:244
  257.4 12.7 %add_convert_fusion = bf16[1024,2048]{1,0:T(8,128)(2,1)} fusion(f32[1024,2048]{1,0:T(8,128)} %fusion.129, bf16[1024,1536]{0,1:T(8,128)(2,1)S(1)} %bitcast.234, bf16[2048,1536]{0,1:T(8,128)(2,1)} %bitcast.255), kind=kOutput, calls=%fused_computation.111 | convolution fusion | flops 6446645248 | bytes 22020096 | tf_op jit(solution)/shard_map/dot_general | solution.py:240
  272.7 6.5 fusion.148
  279.3 12.6 %fusion.121 = f32[2048,3,512]{2,0,1:T(8,128)} fusion(bf16[3,512,1024]{2,1,0:T(8,128)(2,1)} %bitcast.235, bf16[1024,2048]{1,0:T(8,128)(2,1)} %fusion.106), kind=kOutput, calls=%fused_computation.114 | convolution fusion | flops 6442450944 | bytes 19922944 | tf_op jit(solution)/shard_map/dot_general | solution.py:237
  292.0 17.6 %fusion.141 = f32[2048,2048]{1,0:T(8,128)} fusion(bf16[1024,2048]{1,0:T(8,128)(2,1)} %param.31, f32[1024,2048]{1,0:T(8,128)} %fusion.147, f32[2048]{0:T(1024)S(1)} %copy-done.28), kind=kOutput, calls=%fused_computation.174 | convolution fusion | flops 8610906112 | bytes 29368320 | tf_op jit(solution)/shard_map/dot_general | solution.py:212
  309.6 15.3 %fusion.127 = f32[2048,2048]{1,0:T(8,128)} fusion(bf16[1024,2048]{1,0:T(8,128)(2,1)} %fusion.106, bf16[1024,2048]{1,0:T(8,128)(2,1)} %copy-done.36), kind=kOutput, calls=%fused_computation.126 | convolution fusion | flops 8589934592 | bytes 25165824 | tf_op jit(solution)/shard_map/dot_general | solution.py:222
  325.0 15.8 %fusion.142 = f32[1024,2048]{1,0:T(8,128)S(1)} fusion(bf16[2048,2048]{1,0:T(8,128)(2,1)} %all-gather.16.cloned.1.call-done, f32[1024,2048]{1,0:T(8,128)} %fusion.147, f32[2048]{0:T(1024)S(1)} %copy-done.28), kind=kOutput, calls=%fused_computation.175 | convolution fusion | flops 8610906112 | bytes 25174016 | tf_op jit(solution)/shard_map/dot_general | solution.py:191
  348.1 248.8 %collective-permute-done = f32[1024,2048]{1,0:T(8,128)} collective-permute-done((f32[1024,2048]{1,0:T(8,128)S(1)}, f32[1024,2048]{1,0:T(8,128)}, u32[]{:S(2)}, u32[]{:S(2)}) %collective-permute-start) | collective-permute-done | bytes 8388640 | tf_op jit(solution)/shard_map/ppermute | solution.py:198
  596.9 12.3 %add.184 = f32[1024,2048]{1,0:T(8,128)} add(f32[1024,2048]{1,0:T(8,128)} %copy-done.2, f32[1024,2048]{1,0:T(8,128)} %collective-permute-done) | non-fusion elementwise | flops 2097152 | bytes 25165824 | tf_op jit(solution)/shard_map/add | solution.py:198
  614.0 8.9 all-gather.4
  622.9 8.3 all-gather.3
  634.4 6.4 fusion.120
  640.8 331.2 %collective-permute-done.1 = f32[1024,2048]{1,0:T(8,128)} collective-permute-done((f32[1024,2048]{1,0:T(8,128)}, f32[1024,2048]{1,0:T(8,128)}, u32[]{:S(2)}, u32[]{:S(2)}) %collective-permute-start.1) | collective-permute-done | bytes 8388640 | tf_op jit(solution)/shard_map/ppermute | solution.py:198
  971.9 15.5 %convert_reduce_fusion.2 = (f32[2048]{0:T(1024)S(1)}, f32[1024,2048]{1,0:T(8,128)}, bf16[1024,2048]{1,0:T(8,128)(2,1)}) fusion(bf16[1024,2048]{1,0:T(8,128)(2,1)} %param.31, f32[1024]{0:T(1024)S(1)} %broadcast_multiply_fusion.1, f32[1024]{0:T(1024)S(1)} %copy-done.25, bf16[1024,2048]{1,0:T(8,128)(2,1)S(1)} %copy-done.1, ...), kind=kLoop, calls=%fused_computation.89 | loop fusion | flops 35649536 | bytes 41992192 | tf_op jit(solution)/shard_map/reduce_sum | solution.py:210
  987.4 22.9 %all-reduce.8 = (f32[2048]{0:T(1024)S(1)}, f32[2048]{0:T(1024)S(1)}, f32[2,8,64]{2,1,0:T(8,128)S(1)}, f32[8,32]{0,1:T(8,128)S(1)}, f32[2048]{0:T(1024)S(1)}, /*index=5*/f32[32,64]{1,0:T(8,128)S(1)}) all-reduce(f32[2048]{0:T(1024)S(1)} %get-tuple-element.247, ...), channel_id=2, replica_groups=mesh['dp'=8,'tensor'=4] {'dp'}, use_global_device_ids=true, to_apply=%region_15.16.clone | all-reduce | flops 9472 | bytes 75776
  (213 shorter events, 93.7 us)
Async XLA Ops:
  7.2 34.7 %copy-start.31 = (bf16[8,4]{0,1:T(4,128)(2,1)S(1)}, bf16[8,4]{0,1:T(4,128)(2,1)}, u32[]{:S(2)}) copy-start(bf16[8,4]{0,1:T(4,128)(2,1)} %param.24) | copy-start | bytes 196
  7.2 42.7 %copy-start.30 = (bf16[32,8]{0,1:T(8,128)(2,1)S(1)}, bf16[32,8]{0,1:T(8,128)(2,1)}, u32[]{:S(2)}) copy-start(bf16[32,8]{0,1:T(8,128)(2,1)} %param.28) | copy-start | bytes 1540
  7.2 67.2 %all-gather.12.cloned.1.call-start = ((), (), s32[]{:S(2)}) async-start(), calls=%async_computation.5 | async-start | bytes 2359296 | tf_op jit(solution)/shard_map/all_gather | solution.py:123
  7.9 81.4 %all-gather.10.cloned.1.call-start = ((), (), s32[]{:S(2)}) async-start(), calls=%async_computation.4 | async-start | bytes 7077888 | tf_op jit(solution)/shard_map/all_gather | solution.py:120
  10.4 201.3 %all-gather.14.cloned.1.call-start = ((), (), s32[]{:S(2)}) async-start(), calls=%async_computation.6 | async-start | bytes 9437184 | tf_op jit(solution)/shard_map/all_gather | solution.py:125
  11.1 216.1 %all-gather.16.cloned.1.call-start = ((), (), s32[]{:S(2)}) async-start(), calls=%async_computation.7 | async-start | bytes 9437184 | tf_op jit(solution)/shard_map/all_gather | solution.py:127
  11.7 622.7 %all-reduce.11.cloned.1.call-start = ((), (), s32[]{:S(2)}) async-start(), calls=%async_computation.8 | async-start | bytes 8388608 | tf_op jit(solution)/shard_map/psum | solution.py:245
  18.8 61.9 %copy-start.24 = (f32[1024]{0:T(1024)}, f32[1024]{0:T(1024)S(1)}, u32[]{:S(2)}) copy-start(f32[1024]{0:T(1024)S(1)} %broadcast_multiply_fusion.3) | copy-start | bytes 12292
  22.3 58.3 %copy-start.26 = (f32[1024]{0:T(1024)}, f32[1024]{0:T(1024)S(1)}, u32[]{:S(2)}) copy-start(f32[1024]{0:T(1024)S(1)} %add_rsqrt_fusion) | copy-start | bytes 12292
  41.8 38.8 %copy-start.22 = (f32[8,1,256]{2,1,0:T(1,128)}, f32[8,1,256]{2,1,0:T(1,128)S(1)}, u32[]{:S(2)}) copy-start(f32[8,1,256]{2,1,0:T(1,128)S(1)} %convert_element_type.142) | copy-start | bytes 24580
  115.0 88.5 %copy-start.21 = (f32[2,512,16]{1,2,0:T(8,128)S(1)}, f32[2,512,16]{1,2,0:T(8,128)}, u32[]{:S(2)}) copy-start(f32[2,512,16]{1,2,0:T(8,128)} %get-tuple-element.316) | copy-start | bytes 196612
  211.6 45.8 %copy-start.17 = (bf16[192,8,2,512]{3,1,2,0:T(8,128)(2,1)}, bf16[192,8,2,512]{3,1,2,0:T(8,128)(2,1)S(1)}, u32[]{:S(2)}) copy-start(bf16[192,8,2,512]{3,1,2,0:T(8,128)(2,1)S(1)} %copy.149) | copy-start | bytes 9437188
  211.6 15.6 %copy-start.28 = (f32[2048]{0:T(1024)S(1)}, f32[2048]{0:T(1024)}, u32[]{:S(2)}) copy-start(f32[2048]{0:T(1024)} %reshape.385) | copy-start | bytes 24580
  227.2 19.0 %copy-start.32 = (bf16[2048,2048]{1,0:T(8,128)(2,1)S(1)}, bf16[2048,2048]{1,0:T(8,128)(2,1)}, u32[]{:S(2)}) copy-start(bf16[2048,2048]{1,0:T(8,128)(2,1)} %all-gather.14.cloned.1.call-done) | copy-start | bytes 25165828
  246.2 11.2 %copy-start.36 = (bf16[1024,2048]{1,0:T(8,128)(2,1)}, bf16[1024,2048]{1,0:T(8,128)(2,1)S(1)}, u32[]{:S(2)}) copy-start(bf16[1024,2048]{1,0:T(8,128)(2,1)S(1)} %get-tuple-element.294) | copy-start | bytes 12582916
  270.1 743.5 %reduce-scatter.9.cloned.1.call-start = ((), (), s32[]{:S(2)}) async-start(), calls=%async_computation.10 | async-start | bytes 4718592 | tf_op jit(solution)/shard_map/reduce_scatter | solution.py:264
  279.2 734.4 %reduce-scatter.7.cloned.1.call-start = ((), (), s32[]{:S(2)}) async-start(), calls=%async_computation.9 | async-start | bytes 14155776 | tf_op jit(solution)/shard_map/reduce_scatter | solution.py:261
  291.9 721.7 %reduce-scatter.13.cloned.1.call-start = ((), (), s32[]{:S(2)}) async-start(), calls=%async_computation.12 | async-start | bytes 18874368 | tf_op jit(solution)/shard_map/reduce_scatter | solution.py:268
  309.6 704.0 %reduce-scatter.11.cloned.1.call-start = ((), (), s32[]{:S(2)}) async-start(), calls=%async_computation.11 | async-start | bytes 18874368 | tf_op jit(solution)/shard_map/reduce_scatter | solution.py:266
  325.0 15.8 %copy-start.18 = (bf16[512,2048]{1,0:T(8,128)(2,1)S(1)}, bf16[512,2048]{1,0:T(8,128)(2,1)}, u32[]{:S(2)}) copy-start(bf16[512,2048]{1,0:T(8,128)(2,1)} %all-gather.12.cloned.1.call-done) | copy-start | bytes 6291460
  346.7 264.8 %copy-start.35 = (u32[32]{0:T(128)S(1)}, u32[32]{0:T(128)}, u32[]{:S(2)}) copy-start(u32[32]{0:T(128)} %constant.93) | copy-start | bytes 388
  346.7 267.3 %copy-start.33 = (bf16[256]{0:T(256)(128)(2,1)S(1)}, bf16[256]{0:T(256)(128)(2,1)}, u32[]{:S(2)}) copy-start(bf16[256]{0:T(256)(128)(2,1)} %param.26) | copy-start | bytes 1540
  346.7 267.3 %copy-start.34 = (bf16[256]{0:T(256)(128)(2,1)S(1)}, bf16[256]{0:T(256)(128)(2,1)}, u32[]{:S(2)}) copy-start(bf16[256]{0:T(256)(128)(2,1)} %param.30) | copy-start | bytes 1540
  346.7 284.5 %copy-start.12 = (f32[2,1,512,8,64]{2,4,3,1,0:T(8,128)S(1)}, f32[2,1,512,8,64]{2,4,3,1,0:T(8,128)}, u32[]{:S(2)}) copy-start(f32[2,1,512,8,64]{2,4,3,1,0:T(8,128)} %get-tuple-element.109) | copy-start | bytes 6291460
  346.7 286.1 %copy-start.8 = (f32[2,512,8,32]{1,3,2,0:T(8,128)S(1)}, f32[2,512,8,32]{1,3,2,0:T(8,128)}, u32[]{:S(2)}) copy-start(f32[2,512,8,32]{1,3,2,0:T(8,128)} %copy-done.7) | copy-start | bytes 3145732
  346.7 287.7 %copy-start.23 = (f32[8,1,256]{2,1,0:T(1,128)S(1)}, f32[8,1,256]{2,1,0:T(1,128)}, u32[]{:S(2)}) copy-start(f32[8,1,256]{2,1,0:T(1,128)} %copy-done.22) | copy-start | bytes 24580
  346.7 287.7 %copy-start.25 = (f32[1024]{0:T(1024)S(1)}, f32[1024]{0:T(1024)}, u32[]{:S(2)}) copy-start(f32[1024]{0:T(1024)} %copy-done.24) | copy-start | bytes 12292
  346.7 287.6 %copy-start.27 = (f32[1024]{0:T(1024)S(1)}, f32[1024]{0:T(1024)}, u32[]{:S(2)}) copy-start(f32[1024]{0:T(1024)} %copy-done.26) | copy-start | bytes 12292
  346.7 250.2 %collective-permute-start = (f32[1024,2048]{1,0:T(8,128)S(1)}, f32[1024,2048]{1,0:T(8,128)}, u32[]{:S(2)}, u32[]{:S(2)}) collective-permute-start(f32[1024,2048]{1,0:T(8,128)S(1)} %convolution_add_fusion), channel_id=1, source_target_pairs={{0,1},{1,0},{2,3},{3,2},{4,5},{5,4},{6,7},{7,6},{8,9},{9,8},{10,11... | collective-permute-start | bytes 25165832 | tf_op jit(solution)/shard_map/ppermute | solution.py:198
  609.2 362.7 %collective-permute-start.1 = (f32[1024,2048]{1,0:T(8,128)}, f32[1024,2048]{1,0:T(8,128)}, u32[]{:S(2)}, u32[]{:S(2)}) collective-permute-start(f32[1024,2048]{1,0:T(8,128)} %add.184), channel_id=1, source_target_pairs={{0,2},{1,3},{2,0},{3,1},{4,6},{5,7},{6,4},{7,5},{8,10},{9,11},{10,... | collective-permute-start | bytes 25165832 | tf_op jit(solution)/shard_map/ppermute | solution.py:198
  634.4 337.6 %copy-start.1 = (bf16[1024,2048]{1,0:T(8,128)(2,1)S(1)}, bf16[1024,2048]{1,0:T(8,128)(2,1)}, u32[]{:S(2)}) copy-start(bf16[1024,2048]{1,0:T(8,128)(2,1)} %param.18) | copy-start | bytes 12582916
  634.4 337.6 %copy-start.3 = (bf16[1024,2048]{1,0:T(8,128)(2,1)S(1)}, bf16[1024,2048]{1,0:T(8,128)(2,1)}, u32[]{:S(2)}) copy-start(bf16[1024,2048]{1,0:T(8,128)(2,1)} %all-reduce.11.cloned.1.call-done) | copy-start | bytes 12582916
  (24 other events, 80.7 us)
Sparse Core Ops, SparseCore 0:
  9.9 30.8 all-gather.11
  42.6 46.6 all-gather.9
  91.2 54.2 all-gather.13
  147.2 55.8 all-gather.15
  270.2 218.1 all-reduce.10
  492.2 53.5 reduce-scatter.8
  549.8 92.0 reduce-scatter.6
  646.1 115.9 reduce-scatter.12
  766.3 116.1 reduce-scatter.10
